TPU v7x, 32 devices: a whole 2x2x4 slice. The times are simulated.
32 devices in a mesh: groups: 2 (over x), seq: 16 (over z, y, core).
Axes of the slice: x: 2, y: 2, z: 4, core: 2. Of those that a mesh axis runs over, the one named last changes fastest.
Arguments:
- activations: bfloat16 [512, 14336], P(('groups', 'seq')), parts along dimension 0, may hold values from -6 to 6
- out_grads: bfloat16 [512, 2048], P(('groups', 'seq')), parts along dimension 0, may hold values from -6 to 6
- query_ids: int32 [512], P(('groups', 'seq')), parts along dimension 0, may hold values from 0 to 2, never falling along the last dimension, each value on 1 to 128 neighbouring positions
- act_basis: bfloat16 [64, 224, 224], P('seq'), may hold values from -0.375 to 0.375
- grad_basis: bfloat16 [2048, 2048], P(None, 'seq'), may hold values from -0.125 to 0.125
- eigenvalues: float32 [2048, 14336], P(None, 'seq'), may hold values from 8 to 80
Outputs:
- precond: bfloat16 [6, 2048, 14336], P('groups', None, 'seq'), parts along dimension 0
There are 2 independent parts, one for each index of `groups`. A program takes and returns all parts, laid end to end along the dimension named above; an argument that names none is the same for every part. Nothing has to cross between parts.
Inputs may be any that keep to these rules, and one draw needn't show every extreme that they name: `query_ids`: query ids never fall along the tokens; each of the 3 queries has at least one and at most 128 tokens.
All inputs are finite; a program needn't handle non-finite values.
Results may differ from a plain program's by a relative error of at most 0.006.
Values may be sent and summed in bfloat16 or wider, within the bound.
A program may use at most 128 MiB of HBM per device.

v0:
```python
import jax
import jax.numpy as jnp
from jax import lax
from jax.sharding import PartitionSpec as P

QUERIES = 3


def shards(activations, out_grads, query_ids, act_basis, grad_basis, eigenvalues):
    local_blocks = act_basis.shape[0]
    block_order = act_basis.shape[1]
    out_units = grad_basis.shape[0]
    columns = lax.all_to_all(activations, "seq", split_axis=1, concat_axis=0, tiled=True)
    all_tokens = columns.shape[0]
    local_width = local_blocks * block_order
    rotated_act = jnp.einsum(
        "tbi,bik->tbk",
        columns.reshape(all_tokens, local_blocks, block_order),
        act_basis,
        preferred_element_type=jnp.float32,
    )
    rotated_act = rotated_act.astype(jnp.bfloat16).reshape(all_tokens, local_width)
    full_basis = lax.all_gather(grad_basis, "seq", axis=1, tiled=True)
    own_rotated = jnp.dot(out_grads, full_basis, preferred_element_type=jnp.float32).astype(
        jnp.bfloat16
    )
    rotated_grad, token_query = (
        lax.all_gather(own_rotated, "seq", axis=0, tiled=True),
        lax.all_gather(query_ids, "seq", axis=0, tiled=True),
    )
    selector = (token_query[:, None] == jnp.arange(QUERIES, dtype=jnp.int32)[None, :]).astype(
        jnp.bfloat16
    )
    selected = (rotated_act[:, None, :] * selector[:, :, None]).reshape(
        all_tokens, QUERIES * local_width
    )
    moments = lax.dot_general(
        rotated_grad, selected, (((0,), (0,)), ((), ())), preferred_element_type=jnp.float32
    )
    scaled = (moments.reshape(out_units, QUERIES, local_width) / eigenvalues[:, None, :]).astype(
        jnp.bfloat16
    )
    rotated_back = jnp.einsum(
        "dqbk,bik->dqbi",
        scaled.reshape(out_units, QUERIES, local_blocks, block_order),
        act_basis,
        preferred_element_type=jnp.float32,
    )
    rotated_back = rotated_back.astype(jnp.bfloat16).reshape(out_units, QUERIES * local_width)
    result = jnp.dot(full_basis, rotated_back, preferred_element_type=jnp.float32)
    result = result.reshape(out_units, QUERIES, local_width)
    return jnp.transpose(result, (1, 0, 2)).astype(jnp.bfloat16)


def solution(mesh):
    return jax.shard_map(
        shards,
        mesh=mesh,
        in_specs=(
            P(("groups", "seq"), None),
            P(("groups", "seq"), None),
            P(("groups", "seq")),
            P("seq", None, None),
            P(None, "seq"),
            P(None, "seq"),
        ),
        out_specs=P("groups", None, "seq"),
        check_vma=False,
    )
```

profile of v0, /device:TPU:0, one launch (start us, length us, event | category | flops | bytes accessed | tf_op | source)
XLA Modules:
  0.0 207.3 jit_solution(7658103903438815733)
XLA Ops:
  6.5 0.0 copy-start
  6.5 0.0 copy-start.2
  6.5 0.0 all-gather.3.cloned.1.call-start
  6.5 0.7 all-gather.3.cloned.1.call-update
  7.3 0.0 all-gather.5.cloned.1.call-start
  7.3 82.6 %all-gather.3.cloned.1.call-done = bf16[2048,2048]{1,0:T(8,128)(2,1)} async-done(((bf16[2048,128]{1,0:T(8,128)(2,1)}), bf16[2048,2048]{1,0:T(8,128)(2,1)}) %all-gather.3.cloned.1.call-update) | async-done | bytes 8388624 | tf_op jit(solution)/shard_map/all_gather | solution.py:23
  90.0 5.2 %convolution_convert_fusion.1 = bf16[16,2048]{1,0:T(8,128)(2,1)} fusion(bf16[16,2048]{1,0:T(8,128)(2,1)} %param.7, bf16[2048,2048]{1,0:T(8,128)(2,1)} %all-gather.3.cloned.1.call-done), kind=kOutput, calls=%fused_computation.5 | convolution fusion | flops 134250496 | bytes 8519680 | tf_op jit(solution)/shard_map/dot_general | solution.py:24
  95.2 0.0 copy-start.4
  95.2 0.0 copy-start.3
  95.2 0.0 all-gather.5.cloned.1.call-update
  95.2 0.0 copy-done.2
  95.2 0.8 copy.29
  96.0 3.6 %all-to-all-start = ((bf16[16,16,896]{2,0,1:T(8,128)(2,1)}), bf16[16,16,896]{2,0,1:T(8,128)(2,1)S(1)}, u32[]{:S(2)}, u32[]{:S(2)}) async-start(bf16[16,16,896]{2,0,1:T(8,128)(2,1)} %bitcast.36), calls=%async_computation | async-start | bytes 917504 | tf_op jit(solution)/shard_map/all_to_all | solution.py:13
  99.6 8.6 %copy.15 = f32[2048,896]{0,1:T(8,128)} copy(f32[2048,896]{1,0:T(8,128)} %param.11) | data formatting | bytes 14680064 | tf_op args[5]
  108.2 0.0 copy-done.4
  108.2 0.6 dynamic-slice
  109.4 0.0 copy-done.3
  109.4 0.2 dynamic-update-slice
  109.6 12.4 %all-reduce = s32[256]{0:T(256)S(1)} all-reduce(s32[256]{0:T(256)S(1)} %dynamic-update-slice), channel_id=1, replica_groups=mesh['groups'=2,'seq'=16] {'seq'}, use_global_device_ids=true, to_apply=%add | all-reduce | flops 256 | bytes 2048
  122.1 0.0 all-to-all-done
  122.1 0.5 reshape.45
  122.6 0.0 copy-done
  122.6 0.3 convolution_convert_fusion.2
  122.9 10.5 %all-gather.5.cloned.1.call-done = bf16[256,2048]{1,0:T(8,128)(2,1)} async-done(((bf16[16,2048]{1,0:T(8,128)(2,1)}), bf16[256,2048]{1,0:T(8,128)(2,1)}) %all-gather.5.cloned.1.call-update) | async-done | bytes 1048592 | tf_op jit(solution)/shard_map/all_gather | solution.py:28
  133.5 8.2 %divide_convert_fusion = bf16[2048,3,896]{0,2,1:T(8,128)(2,1)} fusion(f32[2048,896]{0,1:T(8,128)} %copy.15, bf16[256,2048]{1,0:T(8,128)(2,1)} %all-gather.5.cloned.1.call-done, bf16[256,3]{0,1:T(4,128)(2,1)S(1)} %fusion.11, bf16[256,896]{0,1:T(8,128)(2,1)S(1)} %bitcast.42), kind=kOutput, calls=%fused_computation | convolution fusion | flops 2832334848 | bytes 19858944 | tf_op jit(solution)/shard_map/dot_general | solution.py:37
  141.6 11.3 %convert_bitcast_fusion = bf16[2048,3,4,224]{0,3,1,2:T(8,128)(2,1)} fusion(bf16[2048,3,4,224]{0,3,2,1:T(8,128)(2,1)} %bitcast.37, bf16[4,224,224]{2,1,0:T(8,128)(2,1)S(1)} %copy-done), kind=kOutput, calls=%fused_computation.4 | convolution fusion | flops 2471755776 | bytes 22421504 | tf_op jit(solution)/shard_map/dqbk,bik->dqbi/dot_general | solution.py:43
  153.0 5.8 %copy.17 = bf16[2048,3,4,224]{0,3,2,1:T(8,128)(2,1)S(1)} copy(bf16[2048,3,4,224]{0,3,1,2:T(8,128)(2,1)} %convert_bitcast_fusion) | data formatting | bytes 22020096 | tf_op jit(solution)/shard_map/convert_element_type | solution.py:49
  158.8 27.0 %convolution_convert_fusion = bf16[2688,2048]{1,0:T(8,128)(2,1)} fusion(bf16[2048,2688]{0,1:T(8,128)(2,1)S(1)} %bitcast.38, bf16[2048,2048]{1,0:T(8,128)(2,1)} %all-gather.3.cloned.1.call-done), kind=kOutput, calls=%fused_computation.1 | convolution fusion | flops 22554083328 | bytes 30408704 | tf_op jit(solution)/shard_map/dot_general | solution.py:50
  185.8 0.0 copy-start.1
  185.8 14.7 %copy.18 = bf16[2048,3,896]{2,0,1:T(8,128)(2,1)} copy(bf16[2048,3,896]{0,2,1:T(8,128)(2,1)} %bitcast.39) | data formatting | bytes 22020096 | tf_op jit(solution)/shard_map/convert_element_type | solution.py:52
  200.5 0.0 copy-done.1
  (2 shorter events, 0.0 us)
Async XLA Ops:
  6.5 116.0 %copy-start = (bf16[4,224,224]{2,1,0:T(8,128)(2,1)S(1)}, bf16[4,224,224]{2,1,0:T(8,128)(2,1)}, u32[]{:S(2)}) copy-start(bf16[4,224,224]{2,1,0:T(8,128)(2,1)} %param.9) | copy-start | bytes 1204228
  6.5 88.7 %copy-start.2 = (bf16[16,14336]{1,0:T(8,128)(2,1)S(1)}, bf16[16,14336]{1,0:T(8,128)(2,1)}, u32[]{:S(2)}) copy-start(bf16[16,14336]{1,0:T(8,128)(2,1)} %param.6) | copy-start | bytes 1376260
  6.5 83.4 %all-gather.3.cloned.1.call-start = ((), (), s32[]{:S(2)}) async-start(), calls=%async_computation.1 | async-start | bytes 8912896 | tf_op jit(solution)/shard_map/all_gather | solution.py:23
  7.3 126.2 %all-gather.5.cloned.1.call-start = ((), (), s32[]{:S(2)}) async-start(), calls=%async_computation.2 | async-start | bytes 1114112 | tf_op jit(solution)/shard_map/all_gather | solution.py:28
  95.2 13.0 %copy-start.4 = (u32[32]{0:T(128)S(1)}, u32[32]{0:T(128)}, u32[]{:S(2)}) copy-start(u32[32]{0:T(128)} %constant.6) | copy-start | bytes 388
  95.2 14.2 %copy-start.3 = (s32[16]{0:T(128)S(1)}, s32[16]{0:T(128)}, u32[]{:S(2)}) copy-start(s32[16]{0:T(128)} %param.8) | copy-start | bytes 196
  96.0 26.0 %all-to-all-start = ((bf16[16,16,896]{2,0,1:T(8,128)(2,1)}), bf16[16,16,896]{2,0,1:T(8,128)(2,1)S(1)}, u32[]{:S(2)}, u32[]{:S(2)}) async-start(bf16[16,16,896]{2,0,1:T(8,128)(2,1)} %bitcast.36), calls=%async_computation | async-start | bytes 917504 | tf_op jit(solution)/shard_map/all_to_all | solution.py:13
  185.8 14.7 %copy-start.1 = (bf16[4,224,224]{2,1,0:T(8,128)(2,1)S(1)}, bf16[4,224,224]{2,1,0:T(8,128)(2,1)}, u32[]{:S(2)}) copy-start(bf16[4,224,224]{2,1,0:T(8,128)(2,1)} %param.9) | copy-start | bytes 1204228
Sparse Core Ops, SparseCore 0:
  9.5 80.4 all-gather.2
  95.3 38.0 all-gather.4
where the time goes:
time: 208 us; the launch traced here: 207 us
  waiting for transfers between devices  93.9 us (45%)
  matrix products  52.1 us (25%)
  local copies, waits for them, and re-layouts  31.2 us (15%)
  between operations  14 us (7%)
  blocking collectives  12.4 us (6%)
  starting transfers between devices  3.6 us (2%)
    all_gather x1, waiting for transfers between devices, shards(): full_basis = lax.all_gather(grad_basis, 'seq', axis=1, tiled=True)  82.6 us
    dot_general x1, matrix products, shards(): jnp.dot(full_basis, rotated_back, preferred_element_type=jnp.float32)  27 us
    convert_element_type x1, local copies, waits for them, and re-layouts, shards(): return jnp.transpose(result, (1, 0, 2)).astype(jnp.bfloat16)  14.7 us
    unnamed x1, blocking collectives  12.4 us
    dot_general x1, matrix products, shards(): jnp.einsum('dqbk,bik->dqbi', scaled.reshape(out_units, QUERIES, local_blo...  11.3 us
    all_gather x1, waiting for transfers between devices, shards(): lax.all_gather(own_rotated, 'seq', axis=0, tiled=True)  10.5 us
    unnamed x14, local copies, waits for them, and re-layouts  9.46 us
    dot_general x1, matrix products, shards(): lax.dot_general(rotated_grad, selected, (((0,), (0,)), ((), ())), preferr...  8.18 us
  transfers between devices with their start and end apart: 3, of which 2 were waited for; matrix products, arithmetic and copies ran while one was open for 5% of the time, Pallas kernels for 0%

commit v1 on v0

--- a/solution.py
+++ b/solution.py
@@ -20,7 +20,7 @@
         preferred_element_type=jnp.float32,
     )
     rotated_act = rotated_act.astype(jnp.bfloat16).reshape(all_tokens, local_width)
-    full_basis = lax.all_gather(grad_basis, "seq", axis=1, tiled=True)
+    full_basis = jnp.concatenate(lax.all_gather(grad_basis, "seq"), axis=1)
     own_rotated = jnp.dot(out_grads, full_basis, preferred_element_type=jnp.float32).astype(
         jnp.bfloat16
     )

time: 208 us -> 220 us (1.058)
  local copies, waits for them, and re-layouts: 31.2 us -> 43.5 us
  waiting for transfers between devices: 93.9 us -> 90.5 us
  matrix products: 52.1 us -> 54.4 us
    reshape x0 -> x1, local copies, waits for them, and re-layouts: none -> 12.3 us  [shards(): full_basis = jnp.concatenate(lax.all_gather(grad_basis, 'seq'), axis=1)]
    all_gather x1, waiting for transfers between devices: 82.6 us -> 79.2 us  [shards(): full_basis = jnp.concatenate(lax.all_gather(grad_basis, 'seq'), axis=1)]
    unnamed x14 -> x16, local copies, waits for them, and re-layouts: 9.46 us -> 9.48 us
where the time goes in v1:
time: 220 us; the launch traced here: 219 us
  waiting for transfers between devices  90.5 us (41%)
  matrix products  54.4 us (25%)
  local copies, waits for them, and re-layouts  43.5 us (20%)
  between operations  14.1 us (6%)
  blocking collectives  12.4 us (6%)
  starting transfers between devices  3.6 us (2%)
    all_gather x1, waiting for transfers between devices, shards(): full_basis = jnp.concatenate(lax.all_gather(grad_basis, 'seq'), axis=1)  79.2 us
    dot_general x1, matrix products, shards(): jnp.dot(full_basis, rotated_back, preferred_element_type=jnp.float32)  28.2 us
    convert_element_type x1, local copies, waits for them, and re-layouts, shards(): return jnp.transpose(result, (1, 0, 2)).astype(jnp.bfloat16)  14.7 us
    unnamed x1, blocking collectives  12.4 us
    reshape x1, local copies, waits for them, and re-layouts, shards(): full_basis = jnp.concatenate(lax.all_gather(grad_basis, 'seq'), axis=1)  12.3 us
    dot_general x1, matrix products, shards(): jnp.einsum('dqbk,bik->dqbi', scaled.reshape(out_units, QUERIES, local_blo...  11.3 us
    all_gather x1, waiting for transfers between devices, shards(): lax.all_gather(own_rotated, 'seq', axis=0, tiled=True)  10.5 us
    unnamed x16, local copies, waits for them, and re-layouts  9.48 us
  transfers between devices with their start and end apart: 3, of which 2 were waited for; matrix products, arithmetic and copies ran while one was open for 5% of the time, Pallas kernels for 0%

profile of v1, /device:TPU:0, one launch (start us, length us, event | category | flops | bytes accessed | tf_op | source)
XLA Modules:
  0.0 218.6 jit_solution(16173889708742890140)
XLA Ops:
  6.5 0.0 copy-start
  6.5 0.0 copy-start.3
  6.5 0.0 all-gather.6.cloned.1.call-start
  6.5 0.7 all-gather.6.cloned.1.call-update
  7.3 0.0 all-gather.4.cloned.1.call-start
  7.3 79.2 %all-gather.6.cloned.1.call-done = bf16[32768,128]{1,0:T(8,128)(2,1)} async-done(((bf16[2048,128]{1,0:T(8,128)(2,1)}), bf16[32768,128]{1,0:T(8,128)(2,1)}) %all-gather.6.cloned.1.call-update) | async-done | bytes 8388624 | tf_op jit(solution)/shard_map/all_gather | solution.py:23
  86.5 0.0 copy-start.2
  86.6 12.3 %copy.19 = bf16[2048,16,128]{0,2,1:T(8,128)(2,1)} copy(bf16[2048,16,128]{2,0,1:T(8,128)(2,1)} %bitcast.46) | data formatting | bytes 16777216 | tf_op jit(solution)/shard_map/reshape | solution.py:23
  98.9 0.0 copy-done.3
  98.9 0.0 copy-start.5
  98.9 0.0 copy-start.4
  98.9 6.3 %convolution_convert_fusion.1 = bf16[16,2048]{1,0:T(8,128)(2,1)} fusion(bf16[16,2048]{1,0:T(8,128)(2,1)S(1)} %copy-done.3, bf16[2048,2048]{0,1:T(8,128)(2,1)} %bitcast.41), kind=kOutput, calls=%fused_computation.5 | convolution fusion | flops 134250496 | bytes 8519680 | tf_op jit(solution)/shard_map/dot_general | solution.py:24
  105.2 0.0 all-gather.4.cloned.1.call-update
  105.2 0.0 copy-done.2
  105.2 0.8 copy.37
  106.0 3.6 %all-to-all-start = ((bf16[16,16,896]{2,0,1:T(8,128)(2,1)}), bf16[16,16,896]{2,0,1:T(8,128)(2,1)S(1)}, u32[]{:S(2)}, u32[]{:S(2)}) async-start(bf16[16,16,896]{2,0,1:T(8,128)(2,1)} %bitcast.40), calls=%async_computation | async-start | bytes 917504 | tf_op jit(solution)/shard_map/all_to_all | solution.py:13
  109.6 8.6 %copy.23 = f32[2048,896]{0,1:T(8,128)} copy(f32[2048,896]{1,0:T(8,128)} %param.11) | data formatting | bytes 14680064 | tf_op args[5]
  118.2 0.0 copy-done.5
  118.2 0.6 dynamic-slice
  119.4 0.0 copy-done.4
  119.4 0.2 dynamic-update-slice
  119.7 12.4 %all-reduce = s32[256]{0:T(256)S(1)} all-reduce(s32[256]{0:T(256)S(1)} %dynamic-update-slice), channel_id=1, replica_groups=mesh['groups'=2,'seq'=16] {'seq'}, use_global_device_ids=true, to_apply=%add | all-reduce | flops 256 | bytes 2048
  132.1 0.0 all-to-all-done
  132.1 0.5 reshape.53
  132.6 0.0 copy-done
  132.6 0.3 convolution_convert_fusion.2
  133.0 10.5 %all-gather.4.cloned.1.call-done = bf16[256,2048]{1,0:T(8,128)(2,1)} async-done(((bf16[16,2048]{1,0:T(8,128)(2,1)}), bf16[256,2048]{1,0:T(8,128)(2,1)}) %all-gather.4.cloned.1.call-update) | async-done | bytes 1048592 | tf_op jit(solution)/shard_map/all_gather | solution.py:28
  143.5 8.2 %divide_convert_fusion = bf16[2048,3,896]{0,2,1:T(8,128)(2,1)} fusion(f32[2048,896]{0,1:T(8,128)} %copy.23, bf16[256,2048]{1,0:T(8,128)(2,1)} %all-gather.4.cloned.1.call-done, bf16[256,3]{0,1:T(4,128)(2,1)S(1)} %fusion.11, bf16[256,896]{0,1:T(8,128)(2,1)S(1)} %bitcast.49), kind=kOutput, calls=%fused_computation | convolution fusion | flops 2832334848 | bytes 19858944 | tf_op jit(solution)/shard_map/dot_general | solution.py:37
  151.7 11.3 %convert_bitcast_fusion = bf16[2048,3,4,224]{0,3,1,2:T(8,128)(2,1)} fusion(bf16[2048,3,4,224]{0,3,2,1:T(8,128)(2,1)} %bitcast.43, bf16[4,224,224]{2,1,0:T(8,128)(2,1)S(1)} %copy-done), kind=kOutput, calls=%fused_computation.4 | convolution fusion | flops 2471755776 | bytes 22421504 | tf_op jit(solution)/shard_map/dqbk,bik->dqbi/dot_general | solution.py:43
  163.0 5.8 %copy.25 = bf16[2048,3,4,224]{0,3,2,1:T(8,128)(2,1)S(1)} copy(bf16[2048,3,4,224]{0,3,1,2:T(8,128)(2,1)} %convert_bitcast_fusion) | data formatting | bytes 22020096 | tf_op jit(solution)/shard_map/convert_element_type | solution.py:49
  168.8 28.2 %convolution_convert_fusion = bf16[2688,2048]{1,0:T(8,128)(2,1)} fusion(bf16[2048,2688]{0,1:T(8,128)(2,1)S(1)} %bitcast.44, bf16[2048,2048]{0,1:T(8,128)(2,1)} %bitcast.42), kind=kOutput, calls=%fused_computation.1 | convolution fusion | flops 22554083328 | bytes 30408704 | tf_op jit(solution)/shard_map/dot_general | solution.py:50
  197.0 0.0 copy-start.1
  197.0 14.7 %copy.26 = bf16[2048,3,896]{2,0,1:T(8,128)(2,1)} copy(bf16[2048,3,896]{0,2,1:T(8,128)(2,1)} %bitcast.45) | data formatting | bytes 22020096 | tf_op jit(solution)/shard_map/convert_element_type | solution.py:52
  211.8 0.0 copy-done.1
  (2 shorter events, 0.0 us)
Async XLA Ops:
  6.5 126.1 %copy-start = (bf16[4,224,224]{2,1,0:T(8,128)(2,1)S(1)}, bf16[4,224,224]{2,1,0:T(8,128)(2,1)}, u32[]{:S(2)}) copy-start(bf16[4,224,224]{2,1,0:T(8,128)(2,1)} %param.9) | copy-start | bytes 1204228
  6.5 92.3 %copy-start.3 = (bf16[16,2048]{1,0:T(8,128)(2,1)S(1)}, bf16[16,2048]{1,0:T(8,128)(2,1)}, u32[]{:S(2)}) copy-start(bf16[16,2048]{1,0:T(8,128)(2,1)} %param.7) | copy-start | bytes 196612
  6.5 80.0 %all-gather.6.cloned.1.call-start = ((), (), s32[]{:S(2)}) async-start(), calls=%async_computation.2 | async-start | bytes 8912896 | tf_op jit(solution)/shard_map/all_gather | solution.py:23
  7.3 136.2 %all-gather.4.cloned.1.call-start = ((), (), s32[]{:S(2)}) async-start(), calls=%async_computation.1 | async-start | bytes 1114112 | tf_op jit(solution)/shard_map/all_gather | solution.py:28
  86.5 18.6 %copy-start.2 = (bf16[16,14336]{1,0:T(8,128)(2,1)S(1)}, bf16[16,14336]{1,0:T(8,128)(2,1)}, u32[]{:S(2)}) copy-start(bf16[16,14336]{1,0:T(8,128)(2,1)} %param.6) | copy-start | bytes 1376260
  98.9 19.3 %copy-start.5 = (u32[32]{0:T(128)S(1)}, u32[32]{0:T(128)}, u32[]{:S(2)}) copy-start(u32[32]{0:T(128)} %constant.6) | copy-start | bytes 388
  98.9 20.6 %copy-start.4 = (s32[16]{0:T(128)S(1)}, s32[16]{0:T(128)}, u32[]{:S(2)}) copy-start(s32[16]{0:T(128)} %param.8) | copy-start | bytes 196
  106.0 26.1 %all-to-all-start = ((bf16[16,16,896]{2,0,1:T(8,128)(2,1)}), bf16[16,16,896]{2,0,1:T(8,128)(2,1)S(1)}, u32[]{:S(2)}, u32[]{:S(2)}) async-start(bf16[16,16,896]{2,0,1:T(8,128)(2,1)} %bitcast.40), calls=%async_computation | async-start | bytes 917504 | tf_op jit(solution)/shard_map/all_to_all | solution.py:13
  197.0 14.7 %copy-start.1 = (bf16[4,224,224]{2,1,0:T(8,128)(2,1)S(1)}, bf16[4,224,224]{2,1,0:T(8,128)(2,1)}, u32[]{:S(2)}) copy-start(bf16[4,224,224]{2,1,0:T(8,128)(2,1)} %param.9) | copy-start | bytes 1204228
Sparse Core Ops, SparseCore 0:
  9.5 77.0 all-gather.5
  105.3 38.1 all-gather.3
